TPU v7x, 32 devices: a whole 2x2x4 slice. The times are simulated.
32 devices in a mesh: dp: 8 (over z, core), expert: 4 (over y, x).
Axes of the slice: x: 2, y: 2, z: 4, core: 2. Of those that a mesh axis runs over, the one named last changes fastest.
Arguments:
- tokens: bfloat16 [24576, 768], P(('dp', 'expert')), may hold values from -6 to 6
- cotangent: bfloat16 [24576, 768], P(('dp', 'expert')), may hold values from -6 to 6
- expert_ids: int32 [24576, 2], P(('dp', 'expert')), may hold values from 0 to 15, all different within a row
- route_gates: float32 [24576, 2], P(('dp', 'expert')), may hold values from 0.25 to 1
- slot_order: int32 [32, 1536], P(('dp', 'expert')), may hold values from 0 to 1535, each once within a row
- prefix_len: int32 [32], P(('dp', 'expert')), may hold values from 1 to 767
- attention_gain: float32 [768], replicated, may hold values from 0.1 to 1.9
- qkv_weight: bfloat16 [768, 2304], replicated, may hold values from -0.21875 to 0.21875
- output_weight: bfloat16 [768, 768], replicated, may hold values from -0.875 to 0.875
- feedforward_gain: float32 [768], replicated, may hold values from 0.1 to 1.9
- shared_gate: bfloat16 [768, 2048], replicated, may hold values from -0.21875 to 0.21875
- shared_up: bfloat16 [768, 2048], replicated, may hold values from -0.21875 to 0.21875
- shared_down: bfloat16 [2048, 768], replicated, may hold values from -0.125 to 0.125
- expert_gate: bfloat16 [16, 768, 2048], P('expert'), may hold values from -0.21875 to 0.21875
- expert_up: bfloat16 [16, 768, 2048], P('expert'), may hold values from -0.21875 to 0.21875
- expert_down: bfloat16 [16, 2048, 768], P('expert'), may hold values from -0.125 to 0.125
Outputs:
- block_out: bfloat16 [24576, 768], P(('dp', 'expert'))
- tokens_grad: bfloat16 [24576, 768], P(('dp', 'expert'))
- attention_gain_grad: float32 [768], P('dp')
- qkv_weight_grad: float32 [768, 2304], P('dp')
- output_weight_grad: float32 [768, 768], P('dp')
- feedforward_gain_grad: float32 [768], P('dp')
- shared_gate_grad: float32 [768, 2048], P('dp')
- shared_up_grad: float32 [768, 2048], P('dp')
- shared_down_grad: float32 [2048, 768], P('dp')
- expert_gate_grad: float32 [16, 768, 2048], P('expert', 'dp')
- expert_up_grad: float32 [16, 768, 2048], P('expert', 'dp')
- expert_down_grad: float32 [16, 2048, 768], P('expert', 'dp')
Inputs may be any that keep to these rules, and one draw needn't show every extreme that they name: `expert_ids`: each token names two different experts; every expert is named by some token. `slot_order`: each row is a permutation of its sequence's pair numbers 2 p + k.
All inputs are finite; a program needn't handle non-finite values.
Results may differ from a plain program's by a relative error of at most 0.023.
Values may be sent and summed in bfloat16 or wider, within the bound.
A program may use at most 320 MiB of HBM per device.

v0:
```python
import jax
import jax.numpy as jnp
from jax import lax
from jax.sharding import PartitionSpec as P

HEADS = 12
HEAD_DIM = 64
E = 16
CAP = 120
epsilon = 1e-06


def rms_forward(values, gain_vector):
    inverse = lax.rsqrt(jnp.mean(values * values, axis=-1, keepdims=True) + epsilon)
    normed = values * inverse
    return (normed * gain_vector, normed, inverse)


def rms_backward(upstream, gain_vector, normed, inverse):
    scaled = upstream * gain_vector
    gain_grad = jnp.sum(upstream * normed, axis=0)
    row_inner = jnp.mean(scaled * normed, axis=-1, keepdims=True)
    return (inverse * (scaled - normed * row_inner), gain_grad)


def rope_tables(length, head_size):
    positions = jnp.arange(length, dtype=jnp.float32)
    frequency = 10000.0 ** (-jnp.arange(head_size // 2, dtype=jnp.float32) * 2.0 / head_size)
    angles = positions[:, None] * frequency[None, :]
    return (jnp.cos(angles)[:, None, :], jnp.sin(angles)[:, None, :])


def rotate(values, cosine, sine_table):
    half_size = values.shape[-1] // 2
    first_half = values[..., :half_size]
    second = values[..., half_size:]
    return jnp.concatenate(
        [first_half * cosine - second * sine_table, second * cosine + first_half * sine_table],
        axis=-1,
    )


def contract_rows(left_side, right_side):
    return lax.dot_general(
        left_side, right_side, (((0,), (0,)), ((), ())), preferred_element_type=jnp.float32
    )


def contract_last(left_side, right_side):
    return lax.dot_general(
        left_side, right_side, (((1,), (1,)), ((), ())), preferred_element_type=jnp.float32
    )


def silu_slope(pre_values):
    sigmoid_gate = jax.nn.sigmoid(pre_values)
    return sigmoid_gate * (1.0 + pre_values * (1.0 - sigmoid_gate))


def shards(
    tokens,
    cotangent,
    expert_ids,
    route_gates,
    slot_order,
    prefix_len,
    attention_gain,
    qkv_weight,
    output_weight,
    feedforward_gain,
    shared_gate,
    shared_up,
    shared_down,
    expert_gate,
    expert_up,
    expert_down,
):
    length, features = tokens.shape
    local_experts = expert_gate.shape[0]
    groups = lax.axis_size("expert")
    pair_count = 2 * length
    score_scale = HEAD_DIM ** (-0.5)
    pair_expert = expert_ids.reshape(pair_count)
    order_row = slot_order[0]
    sorted_expert = pair_expert[order_row]
    onehot = (sorted_expert[:, None] == jnp.arange(E, dtype=jnp.int32)[None, :]).astype(jnp.int32)
    before = jnp.cumsum(onehot, axis=0) - onehot
    sorted_slot = jnp.sum(before * onehot, axis=1)
    position = jnp.zeros((pair_count,), jnp.int32).at[order_row].set(sorted_slot)
    slot_index = jnp.where(position < CAP, pair_expert * CAP + position, E * CAP)
    pair_table = (
        jnp.full((E * CAP + 1,), pair_count, jnp.int32)
        .at[slot_index]
        .set(jnp.arange(pair_count, dtype=jnp.int32))[: E * CAP]
    )
    token_table = pair_table // 2
    zero_row = jnp.zeros((1, features), jnp.bfloat16)
    resid = tokens.astype(jnp.float32)
    normed_one, unit_one, inverse_one = rms_forward(resid, attention_gain)
    normed_low = normed_one.astype(jnp.bfloat16)
    projected = jnp.dot(normed_low, qkv_weight, preferred_element_type=jnp.float32).reshape(
        length, 3, HEADS, HEAD_DIM
    )
    cosine, sine_table = rope_tables(length, HEAD_DIM)
    queries = rotate(projected[:, 0], cosine, sine_table).astype(jnp.bfloat16)
    key_rows = rotate(projected[:, 1], cosine, sine_table).astype(jnp.bfloat16)
    values = projected[:, 2].astype(jnp.bfloat16)
    row_ids = jnp.arange(length)[:, None]
    col_ids = jnp.arange(length)[None, :]
    visible = ((col_ids <= row_ids) | (col_ids < prefix_len[0]))[None]
    scores = (
        jnp.einsum("qhd,khd->hqk", queries, key_rows, preferred_element_type=jnp.float32)
        * score_scale
    )
    scores = jnp.where(visible, scores, -1e30)
    row_peak = jnp.max(scores, axis=-1, keepdims=True)
    exp_scores = jnp.exp(scores - row_peak)
    row_total = jnp.sum(exp_scores, axis=-1, keepdims=True)
    log_total = row_peak + jnp.log(row_total)
    soft_probs = (exp_scores / row_total).astype(jnp.bfloat16)
    attended = jnp.einsum("hqk,khd->qhd", soft_probs, values, preferred_element_type=jnp.float32)
    attended_low = attended.reshape(length, features).astype(jnp.bfloat16)
    attn_branch = jnp.dot(attended_low, output_weight, preferred_element_type=jnp.float32)
    state = resid + attn_branch
    normed_two, unit_two, inverse_two = rms_forward(state, feedforward_gain)
    normed_two_low = normed_two.astype(jnp.bfloat16)
    gate_pre = jnp.dot(normed_two_low, shared_gate, preferred_element_type=jnp.float32)
    up_pre = jnp.dot(normed_two_low, shared_up, preferred_element_type=jnp.float32)
    shared_hidden = (jax.nn.silu(gate_pre) * up_pre).astype(jnp.bfloat16)
    shared_branch = jnp.dot(shared_hidden, shared_down, preferred_element_type=jnp.float32)
    padded_rows = jnp.concatenate([normed_two_low, zero_row], axis=0)
    outgoing = padded_rows[token_table].reshape(groups, local_experts, CAP, features)
    arrived = lax.all_to_all(outgoing, "expert", split_axis=0, concat_axis=0, tiled=True)
    expert_gate_pre = jnp.einsum(
        "slcd,ldf->slcf", arrived, expert_gate, preferred_element_type=jnp.float32
    )
    expert_up_pre = jnp.einsum(
        "slcd,ldf->slcf", arrived, expert_up, preferred_element_type=jnp.float32
    )
    expert_hidden = (jax.nn.silu(expert_gate_pre) * expert_up_pre).astype(jnp.bfloat16)
    expert_result = jnp.einsum(
        "slcf,lfd->slcd", expert_hidden, expert_down, preferred_element_type=jnp.float32
    ).astype(jnp.bfloat16)
    returned = lax.all_to_all(expert_result, "expert", split_axis=0, concat_axis=0, tiled=True)
    returned_pad = jnp.concatenate([returned.reshape(E * CAP, features), zero_row], axis=0)
    picked = returned_pad[slot_index].astype(jnp.float32).reshape(length, 2, features)
    mixture = jnp.sum(picked * route_gates[:, :, None], axis=1)
    block_out = (state + shared_branch + mixture).astype(jnp.bfloat16)
    upstream = cotangent.astype(jnp.float32)
    pair_grad = (route_gates[:, :, None] * upstream[:, None, :]).reshape(pair_count, features)
    pair_grad_pad = jnp.concatenate([pair_grad, jnp.zeros((1, features), jnp.float32)], axis=0)
    slot_grad = (
        pair_grad_pad[pair_table].astype(jnp.bfloat16).reshape(groups, local_experts, CAP, features)
    )
    slot_grad_in = lax.all_to_all(slot_grad, "expert", split_axis=0, concat_axis=0, tiled=True)
    down_w_grad = jnp.einsum(
        "slcf,slcd->lfd", expert_hidden, slot_grad_in, preferred_element_type=jnp.float32
    )
    expert_hidden_grad = jnp.einsum(
        "slcd,lfd->slcf", slot_grad_in, expert_down, preferred_element_type=jnp.float32
    )
    expert_gate_back = (expert_hidden_grad * expert_up_pre * silu_slope(expert_gate_pre)).astype(
        jnp.bfloat16
    )
    expert_up_back = (expert_hidden_grad * jax.nn.silu(expert_gate_pre)).astype(jnp.bfloat16)
    gate_w_grad = jnp.einsum(
        "slcd,slcf->ldf", arrived, expert_gate_back, preferred_element_type=jnp.float32
    )
    up_w_grad = jnp.einsum(
        "slcd,slcf->ldf", arrived, expert_up_back, preferred_element_type=jnp.float32
    )
    dispatched_grad = jnp.einsum(
        "slcf,ldf->slcd", expert_gate_back, expert_gate, preferred_element_type=jnp.float32
    )
    dispatched_grad = dispatched_grad + jnp.einsum(
        "slcf,ldf->slcd", expert_up_back, expert_up, preferred_element_type=jnp.float32
    )
    sent_back = lax.all_to_all(
        dispatched_grad.astype(jnp.bfloat16), "expert", split_axis=0, concat_axis=0, tiled=True
    )
    expert_sums = (
        lax.psum_scatter(
            gate_w_grad.astype(jnp.bfloat16), "dp", scatter_dimension=1, tiled=True
        ).astype(jnp.float32),
        lax.psum_scatter(
            up_w_grad.astype(jnp.bfloat16), "dp", scatter_dimension=1, tiled=True
        ).astype(jnp.float32),
        lax.psum_scatter(
            down_w_grad.astype(jnp.bfloat16), "dp", scatter_dimension=1, tiled=True
        ).astype(jnp.float32),
    )
    back_pad = jnp.concatenate([sent_back.reshape(E * CAP, features), zero_row], axis=0)
    from_experts = jnp.sum(
        back_pad[slot_index].astype(jnp.float32).reshape(length, 2, features), axis=1
    )
    shared_down_grad = contract_rows(shared_hidden, cotangent)
    shared_hidden_grad = contract_last(cotangent, shared_down)
    gate_back = (shared_hidden_grad * up_pre * silu_slope(gate_pre)).astype(jnp.bfloat16)
    up_back = (shared_hidden_grad * jax.nn.silu(gate_pre)).astype(jnp.bfloat16)
    shared_gate_grad = contract_rows(normed_two_low, gate_back)
    shared_up_grad = contract_rows(normed_two_low, up_back)
    normed_two_grad = (
        contract_last(gate_back, shared_gate) + contract_last(up_back, shared_up) + from_experts
    )
    state_norm_grad, feedforward_gain_grad = rms_backward(
        normed_two_grad, feedforward_gain, unit_two, inverse_two
    )
    state_grad = upstream + state_norm_grad
    branch_grad = state_grad.astype(jnp.bfloat16)
    output_weight_grad = contract_rows(attended_low, branch_grad)
    attended_grad = (
        contract_last(branch_grad, output_weight)
        .astype(jnp.bfloat16)
        .reshape(length, HEADS, HEAD_DIM)
    )
    scores_again = (
        jnp.einsum("qhd,khd->hqk", queries, key_rows, preferred_element_type=jnp.float32)
        * score_scale
    )
    probs_again = jnp.exp(jnp.where(visible, scores_again, -1e30) - log_total)
    values_grad = jnp.einsum(
        "hqk,qhd->khd",
        probs_again.astype(jnp.bfloat16),
        attended_grad,
        preferred_element_type=jnp.float32,
    )
    prob_grad = jnp.einsum(
        "qhd,khd->hqk", attended_grad, values, preferred_element_type=jnp.float32
    )
    row_inner = jnp.sum(prob_grad * probs_again, axis=-1, keepdims=True)
    score_grad = (probs_again * (prob_grad - row_inner)).astype(jnp.bfloat16)
    queries_grad = (
        jnp.einsum("hqk,khd->qhd", score_grad, key_rows, preferred_element_type=jnp.float32)
        * score_scale
    )
    keys_grad = (
        jnp.einsum("hqk,qhd->khd", score_grad, queries, preferred_element_type=jnp.float32)
        * score_scale
    )
    queries_grad = rotate(queries_grad, cosine, -sine_table)
    keys_grad = rotate(keys_grad, cosine, -sine_table)
    projected_grad = (
        jnp.stack([queries_grad, keys_grad, values_grad], axis=1)
        .reshape(length, 3 * features)
        .astype(jnp.bfloat16)
    )
    qkv_weight_grad = contract_rows(normed_low, projected_grad)
    normed_one_grad = contract_last(projected_grad, qkv_weight)
    tokens_norm_grad, attention_gain_grad = rms_backward(
        normed_one_grad, attention_gain, unit_one, inverse_one
    )
    tokens_grad = (state_grad + tokens_norm_grad).astype(jnp.bfloat16)
    partial_sums = (
        lax.psum_scatter(
            attention_gain_grad.astype(jnp.bfloat16), "dp", scatter_dimension=0, tiled=True
        ).astype(jnp.float32),
        lax.psum_scatter(
            qkv_weight_grad.astype(jnp.bfloat16), "dp", scatter_dimension=0, tiled=True
        ).astype(jnp.float32),
        lax.psum_scatter(
            output_weight_grad.astype(jnp.bfloat16), "dp", scatter_dimension=0, tiled=True
        ).astype(jnp.float32),
        lax.psum_scatter(
            feedforward_gain_grad.astype(jnp.bfloat16), "dp", scatter_dimension=0, tiled=True
        ).astype(jnp.float32),
        lax.psum_scatter(
            shared_gate_grad.astype(jnp.bfloat16), "dp", scatter_dimension=0, tiled=True
        ).astype(jnp.float32),
        lax.psum_scatter(
            shared_up_grad.astype(jnp.bfloat16), "dp", scatter_dimension=0, tiled=True
        ).astype(jnp.float32),
        lax.psum_scatter(
            shared_down_grad.astype(jnp.bfloat16), "dp", scatter_dimension=0, tiled=True
        ).astype(jnp.float32),
    )
    dense_sums = (
        lax.psum(partial_sums[0].astype(jnp.bfloat16), "expert").astype(jnp.float32),
        lax.psum(partial_sums[1].astype(jnp.bfloat16), "expert").astype(jnp.float32),
        lax.psum(partial_sums[2].astype(jnp.bfloat16), "expert").astype(jnp.float32),
        lax.psum(partial_sums[3].astype(jnp.bfloat16), "expert").astype(jnp.float32),
        lax.psum(partial_sums[4].astype(jnp.bfloat16), "expert").astype(jnp.float32),
        lax.psum(partial_sums[5].astype(jnp.bfloat16), "expert").astype(jnp.float32),
        lax.psum(partial_sums[6].astype(jnp.bfloat16), "expert").astype(jnp.float32),
    )
    return (
        block_out,
        tokens_grad,
        dense_sums[0],
        dense_sums[1],
        dense_sums[2],
        dense_sums[3],
        dense_sums[4],
        dense_sums[5],
        dense_sums[6],
        expert_sums[0],
        expert_sums[1],
        expert_sums[2],
    )


def solution(mesh):
    return jax.shard_map(
        shards,
        mesh=mesh,
        in_specs=(
            P(("dp", "expert"), None),
            P(("dp", "expert"), None),
            P(("dp", "expert"), None),
            P(("dp", "expert"), None),
            P(("dp", "expert"), None),
            P(("dp", "expert")),
            P(),
            P(),
            P(),
            P(),
            P(),
            P(),
            P(),
            P("expert", None, None),
            P("expert", None, None),
            P("expert", None, None),
        ),
        out_specs=(
            P(("dp", "expert"), None),
            P(("dp", "expert"), None),
            P("dp"),
            P("dp", None),
            P("dp", None),
            P("dp"),
            P("dp", None),
            P("dp", None),
            P("dp", None),
            P("expert", "dp", None),
            P("expert", "dp", None),
            P("expert", "dp", None),
        ),
        check_vma=False,
    )
```

profile of v0, /device:TPU:0, one launch (start us, length us, event | category | flops | bytes accessed | tf_op | source)
XLA Modules:
  0.0 993.0 jit_solution(16320943424098945938)
XLA Ops:
  16.8 12.1 %fusion.85 = (f32[12,768]{1,0:T(8,128)S(1)}, f32[12,768,768]{1,2,0:T(8,128)}) fusion(bf16[768,12,32]{0,2,1:T(8,128)(2,1)S(1)} %get-tuple-element.43, bf16[768,12,32]{0,2,1:T(8,128)(2,1)S(1)} %get-tuple-element.44, bf16[768,12,32]{0,2,1:T(8,128)(2,1)S(1)} %get-tuple-element.38, bf16[768,12,32]{0,2,1:T(8,128)(2,1)S(1)} %get-tuple-element.37, ...), kind=kOutput, calls=%fused_computation.163 | convolution fusion | flops 931912704 | bytes 31297536 | tf_op jit(solution)/shard_map/qhd,khd->hqk/dot_general | solution.py:112
  28.9 11.6 %fusion = f32[12,768]{1,0:T(8,128)S(1)} fusion(f32[12,768,768]{1,2,0:T(8,128)} %get-tuple-element.51, f32[12,768]{1,0:T(8,128)S(1)} %get-tuple-element.50), kind=kLoop, calls=%fused_computation.16 | loop fusion | flops 14146560 | bytes 28385280 | tf_op jit(solution)/shard_map/reduce_sum | solution.py:118
  40.5 12.8 %fusion.55 = bf16[12,64,768]{2,1,0:T(8,128)(2,1)} fusion(f32[12,768,768]{1,2,0:T(8,128)} %get-tuple-element.51, f32[12,768]{1,0:T(8,128)S(1)} %fusion, f32[12,768]{1,0:T(8,128)S(1)} %get-tuple-element.50, f32[768,3,12,64]{0,3,2,1:T(8,128)S(1)} %bitcast.173), kind=kOutput, calls=%fused_computation.101 | convolution fusion | flops 927793152 | bytes 30769152 | tf_op jit(solution)/shard_map/hqk,khd->qhd/dot_general | solution.py:121
  91.2 9.4 reduce-window.6
  122.6 9.9 gather_fusion.1
  163.1 10.5 %gather_fusion.3 = bf16[1920,768]{1,0:T(8,128)(2,1)} fusion(bf16[1537,768]{1,0:T(8,128)(2,1)} %concatenate.32, s32[2048]{0:T(1024)S(1)} %get-tuple-element.58), kind=kCustom, calls=%fused_computation.3 | custom fusion | bytes 5905920 | tf_op jit(solution)/shard_map/gather | solution.py:153
  178.5 14.8 %fusion.17 = f32[4,4,120,2048]{3,2,1,0:T(8,128)} fusion(bf16[4,768,2048]{2,1,0:T(8,128)(2,1)} %param.30, bf16[4,4,120,768]{3,2,1,0:T(8,128)(2,1)} %all-to-all-done), kind=kOutput, calls=%fused_computation.38 | convolution fusion | flops 6039797760 | bytes 31260672 | tf_op jit(solution)/shard_map/slcd,ldf->slcf/dot_general | solution.py:137
  193.3 14.7 %fusion.21 = f32[4,4,120,2048]{3,2,1,0:T(8,128)} fusion(bf16[4,768,2048]{2,1,0:T(8,128)(2,1)} %param.29, bf16[4,4,120,768]{3,2,1,0:T(8,128)(2,1)} %all-to-all-done), kind=kOutput, calls=%fused_computation.42 | convolution fusion | flops 6039797760 | bytes 31260672 | tf_op jit(solution)/shard_map/slcd,ldf->slcf/dot_general | solution.py:134
  213.6 25.5 %fusion.3 = (bf16[4,4,120,2048]{3,2,0,1:T(8,128)(2,1)}, bf16[4,4,120,2048]{3,2,0,1:T(8,128)(2,1)}, bf16[4,4,120,2048]{3,2,0,1:T(8,128)(2,1)}) fusion(f32[4,4,120,2048]{3,2,1,0:T(8,128)} %fusion.17, f32[4,4,120,2048]{3,2,1,0:T(8,128)} %fusion.21, bf16[4,2048,768]{2,1,0:T(8,128)(2,1)} %param.31, bf16[4,4,120,768]{3,2,1,0:T(8,128)(2,1)} %all-to-all-done.2), kind=kOutput, calls=%fused_computation.21 | convolution fusion | flops 6098780160 | bytes 70582272 | tf_op jit(solution)/shard_map/slcd,lfd->slcf/dot_general | solution.py:159
  239.1 14.3 %fusion.15 = f32[4,4,120,768]{3,2,1,0:T(8,128)} fusion(bf16[4,4,120,2048]{3,2,0,1:T(8,128)(2,1)} %get-tuple-element.27, bf16[4,768,2048]{2,1,0:T(8,128)(2,1)} %param.30), kind=kOutput, calls=%fused_computation.36 | convolution fusion | flops 6039797760 | bytes 26345472 | tf_op jit(solution)/shard_map/slcf,ldf->slcd/dot_general | solution.py:175
  253.4 15.1 %fusion.34 = bf16[4,4,120,768]{3,2,0,1:T(8,128)(2,1)} fusion(f32[4,4,120,768]{3,2,1,0:T(8,128)} %fusion.15, bf16[4,4,120,2048]{3,2,0,1:T(8,128)(2,1)} %get-tuple-element.25, bf16[4,768,2048]{2,1,0:T(8,128)(2,1)} %param.29), kind=kOutput, calls=%fused_computation.69 | convolution fusion | flops 6042746880 | bytes 29294592 | tf_op jit(solution)/shard_map/slcf,ldf->slcd/dot_general | solution.py:172
  292.4 18.2 %all-to-all-done.3 = bf16[4,4,120,768]{3,2,1,0:T(8,128)(2,1)} async-done(((bf16[4,4,120,768]{3,2,1,0:T(8,128)(2,1)}), bf16[4,4,120,768]{3,2,1,0:T(8,128)(2,1)}, u32[]{:S(2)}, u32[]{:S(2)}) %all-to-all-start.3) | async-done | bytes 2949152 | tf_op jit(solution)/shard_map/all_to_all | solution.py:178
  314.3 8.9 gather_fusion.4
  329.7 9.4 reduce_sum.104
  355.0 23.3 %multiply_reduce_fusion = (f32[12,768]{1,0:T(8,128)}, f32[12,768,768]{1,2,0:T(8,128)}) fusion(f32[12,768,768]{1,2,0:T(8,128)} %get-tuple-element.51, f32[12,768]{1,0:T(8,128)S(1)} %copy-done.20, bf16[768,12,64]{0,2,1:T(8,128)(2,1)S(1)} %bitcast.175, f32[768,3,12,64]{0,3,2,1:T(8,128)} %bitcast.174), kind=kOutput, calls=%fused_computation.8 | convolution fusion | flops 927194112 | bytes 59056128 | tf_op jit(solution)/shard_map/qhd,khd->hqk/dot_general | solution.py:227
  378.3 23.3 %multiply_convert_fusion = bf16[12,768,768]{1,2,0:T(8,128)(2,1)} fusion(f32[12,768,768]{1,2,0:T(8,128)} %get-tuple-element.56, f32[12,768,768]{1,2,0:T(8,128)} %get-tuple-element.51, f32[12,768]{1,0:T(8,128)} %get-tuple-element.55, f32[12,768]{1,0:T(8,128)} %log_add_fusion), kind=kLoop, calls=%fused_computation.7 | loop fusion | flops 28311552 | bytes 70852608 | tf_op jit(solution)/shard_map/convert_element_type | solution.py:231
  401.6 11.2 %multiply_bitcast_fusion = f32[768,12,64]{0,2,1:T(8,128)} fusion(bf16[12,768,768]{1,2,0:T(8,128)(2,1)} %multiply_convert_fusion, bf16[768,12,32]{0,2,1:T(8,128)(2,1)} %copy-done.18, bf16[768,12,32]{0,2,1:T(8,128)(2,1)} %copy-done.17), kind=kOutput, calls=%fused_computation.87 | convolution fusion | flops 908918784 | bytes 17694720 | tf_op jit(solution)/shard_map/hqk,qhd->khd/dot_general | solution.py:237
  412.9 9.0 multiply_bitcast_fusion.1
  426.3 11.7 %fusion.56 = bf16[768,1,12,64]{0,3,2,1:T(8,128)(2,1)S(1)} fusion(bf16[768,12,64]{0,2,1:T(8,128)(2,1)S(1)} %bitcast.176, f32[12,768,768]{1,2,0:T(8,128)} %get-tuple-element.51, f32[12,768]{1,0:T(8,128)S(1)} %copy-done.21), kind=kOutput, calls=%fused_computation.102 | convolution fusion | flops 920715264 | bytes 30707712 | tf_op jit(solution)/shard_map/hqk,qhd->khd/dot_general | solution.py:221
  445.3 9.8 reduce-scatter.11.cloned.1.call-done
  455.1 44.2 %reduce-scatter.9.cloned.1.call-done = bf16[96,2304]{1,0:T(8,128)(2,1)} async-done(((bf16[768,2304]{1,0:T(8,128)(2,1)}), bf16[96,2304]{1,0:T(8,128)(2,1)}) %reduce-scatter.9.cloned.1.call-update) | async-done | bytes 442384 | tf_op jit(solution)/shard_map/reduce_scatter | solution.py:257
  499.4 13.0 %bitcast_convert_fusion = bf16[4,2048,768]{2,1,0:T(8,128)(2,1)} fusion(bf16[4,4,120,2048]{3,2,0,1:T(8,128)(2,1)} %get-tuple-element.26, bf16[4,4,120,768]{3,2,1,0:T(8,128)(2,1)} %all-to-all-done.2), kind=kOutput, calls=%fused_computation.13 | convolution fusion | flops 6046089216 | bytes 23396352 | tf_op jit(solution)/shard_map/slcf,slcd->lfd/dot_general | solution.py:156
  512.4 12.7 %bitcast_convert_fusion.2 = bf16[4,768,2048]{2,1,0:T(8,128)(2,1)} fusion(bf16[4,4,120,768]{3,2,1,0:T(8,128)(2,1)} %all-to-all-done, bf16[4,4,120,2048]{3,2,0,1:T(8,128)(2,1)} %get-tuple-element.25), kind=kOutput, calls=%fused_computation.15 | convolution fusion | flops 6046089216 | bytes 23396352 | tf_op jit(solution)/shard_map/slcd,slcf->ldf/dot_general | solution.py:166
  525.2 13.2 %bitcast_convert_fusion.1 = bf16[4,768,2048]{2,1,0:T(8,128)(2,1)} fusion(bf16[4,4,120,768]{3,2,1,0:T(8,128)(2,1)} %all-to-all-done, bf16[4,4,120,2048]{3,2,0,1:T(8,128)(2,1)} %get-tuple-element.27), kind=kOutput, calls=%fused_computation.14 | convolution fusion | flops 6046089216 | bytes 23396352 | tf_op jit(solution)/shard_map/slcd,slcf->ldf/dot_general | solution.py:169
  538.5 12.7 %convert_bitcast_fusion = bf16[4,4,120,768]{3,2,0,1:T(8,128)(2,1)S(1)} fusion(bf16[4,4,120,2048]{3,2,0,1:T(8,128)(2,1)} %get-tuple-element.26, bf16[4,2048,768]{2,1,0:T(8,128)(2,1)} %param.31), kind=kOutput, calls=%fused_computation.70 | convolution fusion | flops 6041272320 | bytes 23396352 | tf_op jit(solution)/shard_map/slcf,lfd->slcd/dot_general | solution.py:141
  559.7 38.6 %all-to-all-done.1 = bf16[4,4,120,768]{3,2,1,0:T(8,128)(2,1)} async-done(((bf16[4,4,120,768]{3,2,1,0:T(8,128)(2,1)}), bf16[4,4,120,768]{3,2,1,0:T(8,128)(2,1)}, u32[]{:S(2)}, u32[]{:S(2)}) %all-to-all-start.1) | async-done | bytes 2949152 | tf_op jit(solution)/shard_map/all_to_all | solution.py:144
  625.6 18.0 %all-reduce.6 = (bf16[768]{0:T(1024)(128)(2,1)}, bf16[768]{0:T(1024)(128)(2,1)}) all-reduce(bf16[768]{0:T(1024)(128)(2,1)} %get-tuple-element.14, bf16[768]{0:T(1024)(128)(2,1)S(1)} %copy-done.39), channel_id=2, replica_groups=mesh['dp'=8,'expert'=4] {'dp'}, use_global_device_ids=true, to_apply=%region_15.16.clone | all-reduce | flops 1536 | bytes 6144
  645.6 9.7 all-reduce.7
  662.2 9.7 multiply_reduce_fusion.1
  687.3 35.5 %reduce-scatter.23.cloned.1.call-done = bf16[4,256,768]{2,1,0:T(8,128)(2,1)} async-done(((bf16[4,2048,768]{2,1,0:T(8,128)(2,1)}), bf16[4,256,768]{2,1,0:T(8,128)(2,1)}) %reduce-scatter.23.cloned.1.call-update) | async-done | bytes 1572880 | tf_op jit(solution)/shard_map/reduce_scatter | solution.py:188
  726.1 126.7 %reduce-scatter.19.cloned.1.call-done = bf16[4,96,2048]{2,1,0:T(8,128)(2,1)} async-done(((bf16[4,768,2048]{2,1,0:T(8,128)(2,1)}), bf16[4,96,2048]{2,1,0:T(8,128)(2,1)}) %reduce-scatter.19.cloned.1.call-update) | async-done | bytes 1572880 | tf_op jit(solution)/shard_map/reduce_scatter | solution.py:182
  856.2 126.6 %reduce-scatter.21.cloned.1.call-done = bf16[4,96,2048]{2,1,0:T(8,128)(2,1)} async-done(((bf16[4,768,2048]{2,1,0:T(8,128)(2,1)}), bf16[4,96,2048]{2,1,0:T(8,128)(2,1)}) %reduce-scatter.21.cloned.1.call-update) | async-done | bytes 1572880 | tf_op jit(solution)/shard_map/reduce_scatter | solution.py:185
  (196 shorter events, 240.7 us)
Async XLA Ops:
  7.2 438.0 %reduce-scatter.13.cloned.1.call-start = ((), (), s32[]{:S(2)}) async-start(), calls=%async_computation.14 | async-start | bytes 3538944 | tf_op jit(solution)/shard_map/reduce_scatter | solution.py:266
  15.5 25.0 %copy-start.4 = (f32[768,2304]{0,1:T(8,128)}, f32[768,2304]{0,1:T(8,128)S(1)}, u32[]{:S(2)}) copy-start(f32[768,2304]{0,1:T(8,128)S(1)} %fusion.66) | copy-start | bytes 21233668
  16.7 12.1 %copy-start.13 = (bf16[768,12,32]{0,2,1:T(8,128)(2,1)}, bf16[768,12,32]{0,2,1:T(8,128)(2,1)S(1)}, u32[]{:S(2)}) copy-start(bf16[768,12,32]{0,2,1:T(8,128)(2,1)S(1)} %get-tuple-element.43) | copy-start | bytes 1769476
  16.7 12.1 %copy-start.15 = (bf16[768,12,32]{0,2,1:T(8,128)(2,1)}, bf16[768,12,32]{0,2,1:T(8,128)(2,1)S(1)}, u32[]{:S(2)}) copy-start(bf16[768,12,32]{0,2,1:T(8,128)(2,1)S(1)} %get-tuple-element.44) | copy-start | bytes 1769476
  16.8 12.1 %copy-start.17 = (bf16[768,12,32]{0,2,1:T(8,128)(2,1)}, bf16[768,12,32]{0,2,1:T(8,128)(2,1)S(1)}, u32[]{:S(2)}) copy-start(bf16[768,12,32]{0,2,1:T(8,128)(2,1)S(1)} %get-tuple-element.37) | copy-start | bytes 1769476
  16.8 12.1 %copy-start.18 = (bf16[768,12,32]{0,2,1:T(8,128)(2,1)}, bf16[768,12,32]{0,2,1:T(8,128)(2,1)S(1)}, u32[]{:S(2)}) copy-start(bf16[768,12,32]{0,2,1:T(8,128)(2,1)S(1)} %get-tuple-element.38) | copy-start | bytes 1769476
  28.9 11.6 %copy-start.24 = (f32[12,768]{1,0:T(8,128)}, f32[12,768]{1,0:T(8,128)S(1)}, u32[]{:S(2)}) copy-start(f32[12,768]{1,0:T(8,128)S(1)} %get-tuple-element.50) | copy-start | bytes 110596
  40.5 12.9 %copy-start.25 = (f32[12,768]{1,0:T(8,128)}, f32[12,768]{1,0:T(8,128)S(1)}, u32[]{:S(2)}) copy-start(f32[12,768]{1,0:T(8,128)S(1)} %fusion) | copy-start | bytes 110596
  40.5 12.9 %copy-start.8 = (bf16[768,768]{1,0:T(8,128)(2,1)S(1)}, bf16[768,768]{1,0:T(8,128)(2,1)}, u32[]{:S(2)}) copy-start(bf16[768,768]{1,0:T(8,128)(2,1)} %param.16) | copy-start | bytes 3538948
  40.5 12.9 %copy-start.43 = (bf16[768,768]{1,0:T(8,128)(2,1)S(1)}, bf16[768,768]{1,0:T(8,128)(2,1)}, u32[]{:S(2)}) copy-start(bf16[768,768]{1,0:T(8,128)(2,1)} %param.24) | copy-start | bytes 3538948
  58.7 13.1 %copy-start.7 = (bf16[768,768]{1,0:T(8,128)(2,1)}, bf16[768,768]{1,0:T(8,128)(2,1)S(1)}, u32[]{:S(2)}) copy-start(bf16[768,768]{1,0:T(8,128)(2,1)S(1)} %multiply_convert_fusion.4) | copy-start | bytes 3538948
  115.6 7.0 copy-start.28
  132.5 41.1 %all-to-all-start = ((bf16[4,4,120,768]{3,2,1,0:T(8,128)(2,1)}), bf16[4,4,120,768]{3,2,1,0:T(8,128)(2,1)}, u32[]{:S(2)}, u32[]{:S(2)}) async-start(bf16[4,4,120,768]{3,2,1,0:T(8,128)(2,1)} %bitcast.170), calls=%async_computation | async-start | bytes 5898240 | tf_op jit(solution)/shard_map/all_to_all | solution.py:133
  137.6 307.6 %reduce-scatter.15.cloned.1.call-start = ((), (), s32[]{:S(2)}) async-start(), calls=%async_computation.15 | async-start | bytes 3538944 | tf_op jit(solution)/shard_map/reduce_scatter | solution.py:269
  173.6 40.1 %all-to-all-start.2 = ((bf16[4,4,120,768]{3,2,1,0:T(8,128)(2,1)}), bf16[4,4,120,768]{3,2,1,0:T(8,128)(2,1)}, u32[]{:S(2)}, u32[]{:S(2)}) async-start(bf16[4,4,120,768]{3,2,1,0:T(8,128)(2,1)} %bitcast.171), calls=%async_computation.2 | async-start | bytes 5898240 | tf_op jit(solution)/shard_map/all_to_all | solution.py:155
  272.2 38.5 %all-to-all-start.3 = ((bf16[4,4,120,768]{3,2,1,0:T(8,128)(2,1)}), bf16[4,4,120,768]{3,2,1,0:T(8,128)(2,1)}, u32[]{:S(2)}, u32[]{:S(2)}) async-start(bf16[4,4,120,768]{3,2,1,0:T(8,128)(2,1)} %copy.57), calls=%async_computation.3 | async-start | bytes 5898240 | tf_op jit(solution)/shard_map/all_to_all | solution.py:178
  276.8 168.5 %reduce-scatter.17.cloned.1.call-start = ((), (), s32[]{:S(2)}) async-start(), calls=%async_computation.16 | async-start | bytes 3538944 | tf_op jit(solution)/shard_map/reduce_scatter | solution.py:272
  283.4 171.7 %reduce-scatter.11.cloned.1.call-start = ((), (), s32[]{:S(2)}) async-start(), calls=%async_computation.13 | async-start | bytes 1327104 | tf_op jit(solution)/shard_map/reduce_scatter | solution.py:260
  329.6 9.4 copy-start.27
  329.7 9.4 copy-start.32
  339.0 8.6 copy-start.2
  339.0 8.6 copy-start.6
  355.0 23.3 %copy-start.10 = (bf16[768,768]{0,1:T(8,128)(2,1)}, bf16[768,768]{0,1:T(8,128)(2,1)S(1)}, u32[]{:S(2)}) copy-start(bf16[768,768]{0,1:T(8,128)(2,1)S(1)} %convolution_convert_fusion.5) | copy-start | bytes 3538948
  401.6 11.2 %copy-start.14 = (bf16[768,12,32]{0,2,1:T(8,128)(2,1)S(1)}, bf16[768,12,32]{0,2,1:T(8,128)(2,1)}, u32[]{:S(2)}) copy-start(bf16[768,12,32]{0,2,1:T(8,128)(2,1)} %copy-done.13) | copy-start | bytes 1769476
  401.6 11.2 %copy-start.16 = (bf16[768,12,32]{0,2,1:T(8,128)(2,1)S(1)}, bf16[768,12,32]{0,2,1:T(8,128)(2,1)}, u32[]{:S(2)}) copy-start(bf16[768,12,32]{0,2,1:T(8,128)(2,1)} %copy-done.15) | copy-start | bytes 1769476
  421.9 77.4 %reduce-scatter.9.cloned.1.call-start = ((), (), s32[]{:S(2)}) async-start(), calls=%async_computation.12 | async-start | bytes 3981312 | tf_op jit(solution)/shard_map/reduce_scatter | solution.py:257
  445.2 234.6 %all-reduce.11.cloned.1.call-start = ((), (), s32[]{:S(2)}) async-start(), calls=%async_computation.20 | async-start | bytes 3538944 | tf_op jit(solution)/shard_map/psum | solution.py:278
  499.3 223.4 %reduce-scatter.23.cloned.1.call-start = ((), (), s32[]{:S(2)}) async-start(), calls=%async_computation.19 | async-start | bytes 14155776 | tf_op jit(solution)/shard_map/reduce_scatter | solution.py:188
  512.4 340.3 %reduce-scatter.19.cloned.1.call-start = ((), (), s32[]{:S(2)}) async-start(), calls=%async_computation.17 | async-start | bytes 14155776 | tf_op jit(solution)/shard_map/reduce_scatter | solution.py:182
  525.2 457.6 %reduce-scatter.21.cloned.1.call-start = ((), (), s32[]{:S(2)}) async-start(), calls=%async_computation.18 | async-start | bytes 14155776 | tf_op jit(solution)/shard_map/reduce_scatter | solution.py:185
  553.0 45.3 %all-to-all-start.1 = ((bf16[4,4,120,768]{3,2,1,0:T(8,128)(2,1)}), bf16[4,4,120,768]{3,2,1,0:T(8,128)(2,1)}, u32[]{:S(2)}, u32[]{:S(2)}) async-start(bf16[4,4,120,768]{3,2,1,0:T(8,128)(2,1)} %copy.53), calls=%async_computation.1 | async-start | bytes 5898240 | tf_op jit(solution)/shard_map/all_to_all | solution.py:144
  617.9 7.7 copy-start.39
  (26 other events, 71.4 us)
Sparse Core Ops, SparseCore 0:
  78.0 43.0 reduce-scatter.12
  144.5 42.9 reduce-scatter.14
  283.5 42.1 reduce-scatter.16
  422.0 33.0 reduce-scatter.10
  457.3 42.0 reduce-scatter.8
  503.3 87.2 all-reduce.10
  593.0 129.6 reduce-scatter.22
  725.1 127.5 reduce-scatter.18
  855.1 127.5 reduce-scatter.20
where the time goes:
time: 1000 us; the launch traced here: 993 us
  waiting for transfers between devices  405 us (40%)
  matrix products  296 us (30%)
  local copies, waits for them, and re-layouts  122 us (12%)
  other arithmetic  106 us (11%)
  blocking collectives  27.7 us (3%)
  starting transfers between devices  20 us (2%)
  between operations  16.2 us (2%)
    reduce_scatter x1, waiting for transfers between devices, shards(): lax.psum_scatter(gate_w_grad.astype(jnp.bfloat16), 'dp', scatter_dimensio...  127 us
    reduce_scatter x1, waiting for transfers between devices, shards(): lax.psum_scatter(up_w_grad.astype(jnp.bfloat16), 'dp', scatter_dimension=...  127 us
    reduce_scatter x1, waiting for transfers between devices, shards(): lax.psum_scatter(qkv_weight_grad.astype(jnp.bfloat16), 'dp', scatter_dime...  44.2 us
    all_to_all x1, waiting for transfers between devices, shards(): lax.all_to_all(expert_result, 'expert', split_axis=0, concat_axis=0, tile...  38.6 us
    reduce_scatter x1, waiting for transfers between devices, shards(): lax.psum_scatter(down_w_grad.astype(jnp.bfloat16), 'dp', scatter_dimensio...  35.5 us
    dot_general x5, matrix products, contract_last(): lax.dot_general(left_side, right_side, (((1,), (1,)), ((), ())), preferre...  34.1 us
    dot_general x5, matrix products, contract_rows(): lax.dot_general(left_side, right_side, (((0,), (0,)), ((), ())), preferre...  26.1 us
    dot_general x1, matrix products, shards(): jnp.einsum('slcd,lfd->slcf', slot_grad_in, expert_down, preferred_element...  25.5 us
  transfers between devices with their start and end apart: 13, of which 8 were waited for; matrix products, arithmetic and copies ran while one was open for 45% of the time, Pallas kernels for 0%

commit v1 on v0

--- a/solution.py
+++ b/solution.py
@@ -8,6 +8,22 @@
 E = 16
 CAP = 120
 epsilon = 1e-06
+
+
+def swapped_with_each(x, axis, split, join):
+    ways, here = (lax.axis_size(axis), lax.axis_index(axis))
+    width = x.shape[split] // ways
+    dims = list(x.shape)
+    dims[split] = width
+    height = dims[join]
+    dims[join] = height * ways
+    full = jnp.zeros(dims, x.dtype)
+    for mask in range(ways):
+        part = lax.dynamic_slice_in_dim(x, (here ^ mask) * width, width, axis=split)
+        if mask:
+            part = lax.ppermute(part, axis, [(d, d ^ mask) for d in range(ways)])
+        full = lax.dynamic_update_slice_in_dim(full, part, (here ^ mask) * height, axis=join)
+    return full
 
 
 def rms_forward(values, gain_vector):
@@ -175,9 +191,7 @@
     dispatched_grad = dispatched_grad + jnp.einsum(
         "slcf,ldf->slcd", expert_up_back, expert_up, preferred_element_type=jnp.float32
     )
-    sent_back = lax.all_to_all(
-        dispatched_grad.astype(jnp.bfloat16), "expert", split_axis=0, concat_axis=0, tiled=True
-    )
+    sent_back = swapped_with_each(dispatched_grad.astype(jnp.bfloat16), "expert", 0, 0)
     expert_sums = (
         lax.psum_scatter(
             gate_w_grad.astype(jnp.bfloat16), "dp", scatter_dimension=1, tiled=True

time: 1000 us -> 1050 us (1.050)
  waiting for transfers between devices: 405 us -> 445 us
    reduce_scatter x1, waiting for transfers between devices: 0.02 us -> 42.2 us  [shards(): lax.psum_scatter(shared_down_grad.astype(jnp.bfloat16), 'dp', scatter_dim...]
    all_to_all x1, waiting for transfers between devices: 38.6 us -> 0.01 us  [shards(): lax.all_to_all(expert_result, 'expert', split_axis=0, concat_axis=0, tile...]
    reduce_scatter x1, waiting for transfers between devices: 35.5 us -> 70.2 us  [shards(): lax.psum_scatter(down_w_grad.astype(jnp.bfloat16), 'dp', scatter_dimensio...]
    ppermute x0 -> x3, waiting for transfers between devices: none -> 23.9 us  [swapped_with_each(): part = lax.ppermute(part, axis, [(d, d ^ mask) for d in range(ways)])]
    all_to_all x1 -> x0, waiting for transfers between devices: 18.2 us -> none  [shards(): lax.all_to_all(dispatched_grad.astype(jnp.bfloat16), 'expert', split_axis...]
  transfers between devices with their start and end apart: 13 -> 15, of which waited for: 8 -> 8; matrix products, arithmetic and copies ran while one was open for 45% -> 31% of each run, Pallas kernels for 0% -> 0%
where the time goes in v1:
time: 1050 us; the launch traced here: 1040 us
  waiting for transfers between devices  445 us (42%)
  matrix products  303 us (29%)
  local copies, waits for them, and re-layouts  120 us (11%)
  other arithmetic  106 us (10%)
  blocking collectives  32.9 us (3%)
  starting transfers between devices  19.3 us (2%)
  between operations  16.2 us (2%)
    reduce_scatter x1, waiting for transfers between devices, shards(): lax.psum_scatter(gate_w_grad.astype(jnp.bfloat16), 'dp', scatter_dimensio...  127 us
    reduce_scatter x1, waiting for transfers between devices, shards(): lax.psum_scatter(up_w_grad.astype(jnp.bfloat16), 'dp', scatter_dimension=...  127 us
    reduce_scatter x1, waiting for transfers between devices, shards(): lax.psum_scatter(down_w_grad.astype(jnp.bfloat16), 'dp', scatter_dimensio...  70.2 us
    reduce_scatter x1, waiting for transfers between devices, shards(): lax.psum_scatter(qkv_weight_grad.astype(jnp.bfloat16), 'dp', scatter_dime...  45.1 us
    reduce_scatter x1, waiting for transfers between devices, shards(): lax.psum_scatter(shared_down_grad.astype(jnp.bfloat16), 'dp', scatter_dim...  42.2 us
    dot_general x5, matrix products, contract_last(): lax.dot_general(left_side, right_side, (((1,), (1,)), ((), ())), preferre...  34.5 us
    dot_general x5, matrix products, contract_rows(): lax.dot_general(left_side, right_side, (((0,), (0,)), ((), ())), preferre...  26.9 us
    dot_general x1, matrix products, shards(): jnp.einsum('slcd,lfd->slcf', slot_grad_in, expert_down, preferred_element...  25.5 us
  transfers between devices with their start and end apart: 15, of which 8 were waited for; matrix products, arithmetic and copies ran while one was open for 31% of the time, Pallas kernels for 0%

profile of v1, /device:TPU:0, one launch (start us, length us, event | category | flops | bytes accessed | tf_op | source)
XLA Modules:
  0.0 1041.4 jit_solution(3688796533446629247)
XLA Ops:
  25.8 9.4 reduce-window.6
  62.1 12.0 %fusion.84 = (f32[12,768]{1,0:T(8,128)S(1)}, f32[12,768,768]{1,2,0:T(8,128)}) fusion(bf16[768,12,32]{0,2,1:T(8,128)(2,1)S(1)} %get-tuple-element.46, bf16[768,12,32]{0,2,1:T(8,128)(2,1)S(1)} %get-tuple-element.47, bf16[768,12,32]{0,2,1:T(8,128)(2,1)S(1)} %get-tuple-element.41, bf16[768,12,32]{0,2,1:T(8,128)(2,1)S(1)} %get-tuple-element.40, ...), kind=kOutput, calls=%fused_computation.169 | convolution fusion | flops 931912704 | bytes 31297536 | tf_op jit(solution)/shard_map/qhd,khd->hqk/dot_general | solution.py:128
  74.1 11.6 %fusion = f32[12,768]{1,0:T(8,128)S(1)} fusion(f32[12,768,768]{1,2,0:T(8,128)} %get-tuple-element.54, f32[12,768]{1,0:T(8,128)S(1)} %get-tuple-element.53), kind=kLoop, calls=%fused_computation.16 | loop fusion | flops 14146560 | bytes 28385280 | tf_op jit(solution)/shard_map/reduce_sum | solution.py:134
  85.7 12.3 %fusion.54 = bf16[12,64,768]{2,1,0:T(8,128)(2,1)} fusion(f32[12,768,768]{1,2,0:T(8,128)} %get-tuple-element.54, f32[12,768]{1,0:T(8,128)S(1)} %fusion, f32[12,768]{1,0:T(8,128)S(1)} %get-tuple-element.53, f32[768,3,12,64]{0,3,2,1:T(8,128)S(1)} %bitcast.180), kind=kOutput, calls=%fused_computation.100 | convolution fusion | flops 927793152 | bytes 30769152 | tf_op jit(solution)/shard_map/hqk,khd->qhd/dot_general | solution.py:137
  103.6 9.9 gather_fusion.1
  144.4 10.4 gather_fusion.3
  159.8 9.2 multiply_convert_fusion.1
  173.7 15.1 %fusion.17 = f32[4,4,120,2048]{3,2,1,0:T(8,128)} fusion(bf16[4,768,2048]{2,1,0:T(8,128)(2,1)} %param.30, bf16[4,4,120,768]{3,2,1,0:T(8,128)(2,1)} %all-to-all-done), kind=kOutput, calls=%fused_computation.38 | convolution fusion | flops 6039797760 | bytes 31260672 | tf_op jit(solution)/shard_map/slcd,ldf->slcf/dot_general | solution.py:153
  188.8 14.6 %fusion.21 = f32[4,4,120,2048]{3,2,1,0:T(8,128)} fusion(bf16[4,768,2048]{2,1,0:T(8,128)(2,1)} %param.29, bf16[4,4,120,768]{3,2,1,0:T(8,128)(2,1)} %all-to-all-done), kind=kOutput, calls=%fused_computation.42 | convolution fusion | flops 6039797760 | bytes 31260672 | tf_op jit(solution)/shard_map/slcd,ldf->slcf/dot_general | solution.py:150
  208.7 25.5 %fusion.3 = (bf16[4,4,120,2048]{3,2,0,1:T(8,128)(2,1)}, bf16[4,4,120,2048]{3,2,0,1:T(8,128)(2,1)}, bf16[4,4,120,2048]{3,2,0,1:T(8,128)(2,1)}) fusion(f32[4,4,120,2048]{3,2,1,0:T(8,128)} %fusion.17, f32[4,4,120,2048]{3,2,1,0:T(8,128)} %fusion.21, bf16[4,2048,768]{2,1,0:T(8,128)(2,1)} %param.31, bf16[4,4,120,768]{3,2,1,0:T(8,128)(2,1)} %all-to-all-done.2), kind=kOutput, calls=%fused_computation.21 | convolution fusion | flops 6098780160 | bytes 70582272 | tf_op jit(solution)/shard_map/slcd,lfd->slcf/dot_general | solution.py:175
  234.2 14.3 %fusion.15 = f32[4,4,120,768]{3,2,1,0:T(8,128)} fusion(bf16[4,4,120,2048]{3,2,0,1:T(8,128)(2,1)} %get-tuple-element.27, bf16[4,768,2048]{2,1,0:T(8,128)(2,1)} %param.30), kind=kOutput, calls=%fused_computation.36 | convolution fusion | flops 6039797760 | bytes 26345472 | tf_op jit(solution)/shard_map/slcf,ldf->slcd/dot_general | solution.py:191
  248.5 14.9 %add_convert_fusion = bf16[4,4,120,768]{3,2,1,0:T(8,128)(2,1)} fusion(f32[4,4,120,768]{3,2,1,0:T(8,128)} %fusion.15, bf16[4,4,120,2048]{3,2,0,1:T(8,128)(2,1)} %get-tuple-element.25, bf16[4,768,2048]{2,1,0:T(8,128)(2,1)} %param.29), kind=kOutput, calls=%fused_computation.55 | convolution fusion | flops 6042746880 | bytes 29294592 | tf_op jit(solution)/shard_map/slcf,ldf->slcd/dot_general | solution.py:188
  277.4 23.9 %collective-permute-done = bf16[1,4,120,768]{3,2,1,0:T(8,128)(2,1)} collective-permute-done((bf16[1,4,120,768]{3,2,1,0:T(8,128)(2,1)}, bf16[1,4,120,768]{3,2,1,0:T(8,128)(2,1)}, u32[]{:S(2)}, u32[]{:S(2)}) %collective-permute-start) | collective-permute-done | bytes 737312 | tf_op jit(solution)/shard_map/ppermute | solution.py:24
  306.7 9.0 gather_fusion.4
  322.1 9.4 reduce_sum.104
  368.9 23.6 %multiply_reduce_fusion = (f32[12,768]{1,0:T(8,128)}, f32[12,768,768]{1,2,0:T(8,128)}) fusion(f32[12,768,768]{1,2,0:T(8,128)} %get-tuple-element.54, f32[12,768]{1,0:T(8,128)S(1)} %log_add_fusion, bf16[768,12,64]{0,2,1:T(8,128)(2,1)S(1)} %bitcast.182, f32[768,3,12,64]{0,3,2,1:T(8,128)} %bitcast.181), kind=kOutput, calls=%fused_computation.8 | convolution fusion | flops 927194112 | bytes 59056128 | tf_op jit(solution)/shard_map/qhd,khd->hqk/dot_general | solution.py:241
  392.4 24.1 %multiply_convert_fusion = bf16[12,768,768]{1,2,0:T(8,128)(2,1)} fusion(f32[12,768,768]{1,2,0:T(8,128)} %get-tuple-element.59, f32[12,768,768]{1,2,0:T(8,128)} %get-tuple-element.54, f32[12,768]{1,0:T(8,128)} %get-tuple-element.58, f32[12,768]{1,0:T(8,128)} %copy-done.20), kind=kLoop, calls=%fused_computation.7 | loop fusion | flops 28311552 | bytes 70852608 | tf_op jit(solution)/shard_map/convert_element_type | solution.py:245
  416.5 9.9 multiply_bitcast_fusion
  436.4 11.9 %fusion.55 = bf16[768,1,12,64]{0,3,2,1:T(8,128)(2,1)S(1)} fusion(bf16[768,12,64]{0,2,1:T(8,128)(2,1)S(1)} %bitcast.183, f32[12,768,768]{1,2,0:T(8,128)} %get-tuple-element.54, f32[12,768]{1,0:T(8,128)S(1)} %copy-done.21), kind=kOutput, calls=%fused_computation.101 | convolution fusion | flops 920715264 | bytes 30707712 | tf_op jit(solution)/shard_map/hqk,qhd->khd/dot_general | solution.py:235
  460.6 42.2 %reduce-scatter.17.cloned.1.call-done = bf16[256,768]{1,0:T(8,128)(2,1)} async-done(((bf16[2048,768]{1,0:T(8,128)(2,1)}), bf16[256,768]{1,0:T(8,128)(2,1)}) %reduce-scatter.17.cloned.1.call-update) | async-done | bytes 393232 | tf_op jit(solution)/shard_map/reduce_scatter | solution.py:286
  502.8 45.1 %reduce-scatter.9.cloned.1.call-done = bf16[96,2304]{1,0:T(8,128)(2,1)} async-done(((bf16[768,2304]{1,0:T(8,128)(2,1)}), bf16[96,2304]{1,0:T(8,128)(2,1)}) %reduce-scatter.9.cloned.1.call-update) | async-done | bytes 442384 | tf_op jit(solution)/shard_map/reduce_scatter | solution.py:271
  548.0 12.9 %bitcast_convert_fusion = bf16[4,2048,768]{2,1,0:T(8,128)(2,1)} fusion(bf16[4,4,120,2048]{3,2,0,1:T(8,128)(2,1)} %get-tuple-element.26, bf16[4,4,120,768]{3,2,1,0:T(8,128)(2,1)} %all-to-all-done.2), kind=kOutput, calls=%fused_computation.13 | convolution fusion | flops 6046089216 | bytes 23396352 | tf_op jit(solution)/shard_map/slcf,slcd->lfd/dot_general | solution.py:172
  560.9 12.7 %bitcast_convert_fusion.2 = bf16[4,768,2048]{2,1,0:T(8,128)(2,1)} fusion(bf16[4,4,120,768]{3,2,1,0:T(8,128)(2,1)} %all-to-all-done, bf16[4,4,120,2048]{3,2,0,1:T(8,128)(2,1)} %get-tuple-element.25), kind=kOutput, calls=%fused_computation.15 | convolution fusion | flops 6046089216 | bytes 23396352 | tf_op jit(solution)/shard_map/slcd,slcf->ldf/dot_general | solution.py:182
  573.7 13.2 %bitcast_convert_fusion.1 = bf16[4,768,2048]{2,1,0:T(8,128)(2,1)} fusion(bf16[4,4,120,768]{3,2,1,0:T(8,128)(2,1)} %all-to-all-done, bf16[4,4,120,2048]{3,2,0,1:T(8,128)(2,1)} %get-tuple-element.27), kind=kOutput, calls=%fused_computation.14 | convolution fusion | flops 6046089216 | bytes 23396352 | tf_op jit(solution)/shard_map/slcd,slcf->ldf/dot_general | solution.py:185
  587.0 12.7 %convert_bitcast_fusion = bf16[4,4,120,768]{3,2,0,1:T(8,128)(2,1)S(1)} fusion(bf16[4,4,120,2048]{3,2,0,1:T(8,128)(2,1)} %get-tuple-element.26, bf16[4,2048,768]{2,1,0:T(8,128)(2,1)} %param.31), kind=kOutput, calls=%fused_computation.69 | convolution fusion | flops 6041272320 | bytes 23396352 | tf_op jit(solution)/shard_map/slcf,lfd->slcd/dot_general | solution.py:157
  615.3 15.2 %all-reduce.6 = (bf16[768]{0:T(1024)(128)(2,1)}, bf16[768]{0:T(1024)(128)(2,1)}) all-reduce(bf16[768]{0:T(1024)(128)(2,1)} %get-tuple-element.14, bf16[768]{0:T(1024)(128)(2,1)S(1)} %copy-done.40), channel_id=2, replica_groups=mesh['dp'=8,'expert'=4] {'dp'}, use_global_device_ids=true, to_apply=%region_15.16.clone | all-reduce | flops 1536 | bytes 6144
  632.5 17.8 %all-reduce.7 = (bf16[96]{0:T(256)(128)(2,1)}, bf16[96]{0:T(256)(128)(2,1)}) all-reduce(bf16[96]{0:T(256)(128)(2,1)S(1)} %dynamic-slice.17, bf16[96]{0:T(256)(128)(2,1)} %dynamic-slice.19), channel_id=1, replica_groups=mesh['dp'=8,'expert'=4] {'expert'}, use_global_device_ids=true, to_apply=%region_16.17 | all-reduce | flops 192 | bytes 768 | tf_op jit(solution)/shard_map/psum | solution.py:291
  660.7 9.0 gather_fusion.2
  676.0 9.6 multiply_reduce_fusion.1
  701.1 70.2 %reduce-scatter.23.cloned.1.call-done = bf16[4,256,768]{2,1,0:T(8,128)(2,1)} async-done(((bf16[4,2048,768]{2,1,0:T(8,128)(2,1)}), bf16[4,256,768]{2,1,0:T(8,128)(2,1)}) %reduce-scatter.23.cloned.1.call-update) | async-done | bytes 1572880 | tf_op jit(solution)/shard_map/reduce_scatter | solution.py:202
  774.6 126.7 %reduce-scatter.19.cloned.1.call-done = bf16[4,96,2048]{2,1,0:T(8,128)(2,1)} async-done(((bf16[4,768,2048]{2,1,0:T(8,128)(2,1)}), bf16[4,96,2048]{2,1,0:T(8,128)(2,1)}) %reduce-scatter.19.cloned.1.call-update) | async-done | bytes 1572880 | tf_op jit(solution)/shard_map/reduce_scatter | solution.py:196
  904.7 126.6 %reduce-scatter.21.cloned.1.call-done = bf16[4,96,2048]{2,1,0:T(8,128)(2,1)} async-done(((bf16[4,768,2048]{2,1,0:T(8,128)(2,1)}), bf16[4,96,2048]{2,1,0:T(8,128)(2,1)}) %reduce-scatter.21.cloned.1.call-update) | async-done | bytes 1572880 | tf_op jit(solution)/shard_map/reduce_scatter | solution.py:199
  (205 shorter events, 240.5 us)
Async XLA Ops:
  7.2 48.6 %copy-start = (bf16[768,2304]{1,0:T(8,128)(2,1)S(1)}, bf16[768,2304]{1,0:T(8,128)(2,1)}, u32[]{:S(2)}) copy-start(bf16[768,2304]{1,0:T(8,128)(2,1)} %param.23) | copy-start | bytes 10616836
  47.9 12.3 %copy-start.32 = (s32[1536]{0:T(1024)}, s32[1536]{0:T(1024)S(1)}, u32[]{:S(2)}) copy-start(s32[1536]{0:T(1024)S(1)} %compare_select_fusion.2) | copy-start | bytes 18436
  60.2 25.5 %copy-start.4 = (f32[768,2304]{0,1:T(8,128)}, f32[768,2304]{0,1:T(8,128)S(1)}, u32[]{:S(2)}) copy-start(f32[768,2304]{0,1:T(8,128)S(1)} %fusion.65) | copy-start | bytes 21233668
  62.1 12.0 %copy-start.13 = (bf16[768,12,32]{0,2,1:T(8,128)(2,1)}, bf16[768,12,32]{0,2,1:T(8,128)(2,1)S(1)}, u32[]{:S(2)}) copy-start(bf16[768,12,32]{0,2,1:T(8,128)(2,1)S(1)} %get-tuple-element.46) | copy-start | bytes 1769476
  62.1 12.0 %copy-start.15 = (bf16[768,12,32]{0,2,1:T(8,128)(2,1)}, bf16[768,12,32]{0,2,1:T(8,128)(2,1)S(1)}, u32[]{:S(2)}) copy-start(bf16[768,12,32]{0,2,1:T(8,128)(2,1)S(1)} %get-tuple-element.47) | copy-start | bytes 1769476
  62.1 12.0 %copy-start.16 = (bf16[768,12,32]{0,2,1:T(8,128)(2,1)}, bf16[768,12,32]{0,2,1:T(8,128)(2,1)S(1)}, u32[]{:S(2)}) copy-start(bf16[768,12,32]{0,2,1:T(8,128)(2,1)S(1)} %get-tuple-element.40) | copy-start | bytes 1769476
  62.1 12.0 %copy-start.17 = (bf16[768,12,32]{0,2,1:T(8,128)(2,1)}, bf16[768,12,32]{0,2,1:T(8,128)(2,1)S(1)}, u32[]{:S(2)}) copy-start(bf16[768,12,32]{0,2,1:T(8,128)(2,1)S(1)} %get-tuple-element.41) | copy-start | bytes 1769476
  74.1 11.6 %copy-start.26 = (f32[12,768]{1,0:T(8,128)}, f32[12,768]{1,0:T(8,128)S(1)}, u32[]{:S(2)}) copy-start(f32[12,768]{1,0:T(8,128)S(1)} %get-tuple-element.53) | copy-start | bytes 110596
  85.7 12.3 %copy-start.27 = (f32[12,768]{1,0:T(8,128)}, f32[12,768]{1,0:T(8,128)S(1)}, u32[]{:S(2)}) copy-start(f32[12,768]{1,0:T(8,128)S(1)} %fusion) | copy-start | bytes 110596
  85.7 12.3 %copy-start.8 = (bf16[768,768]{1,0:T(8,128)(2,1)S(1)}, bf16[768,768]{1,0:T(8,128)(2,1)}, u32[]{:S(2)}) copy-start(bf16[768,768]{1,0:T(8,128)(2,1)} %param.16) | copy-start | bytes 3538948
  113.5 55.5 %all-to-all-start = ((bf16[4,4,120,768]{3,2,1,0:T(8,128)(2,1)}), bf16[4,4,120,768]{3,2,1,0:T(8,128)(2,1)}, u32[]{:S(2)}, u32[]{:S(2)}) async-start(bf16[4,4,120,768]{3,2,1,0:T(8,128)(2,1)} %bitcast.176), calls=%async_computation | async-start | bytes 5898240 | tf_op jit(solution)/shard_map/all_to_all | solution.py:149
  169.0 39.7 %all-to-all-start.2 = ((bf16[4,4,120,768]{3,2,1,0:T(8,128)(2,1)}), bf16[4,4,120,768]{3,2,1,0:T(8,128)(2,1)}, u32[]{:S(2)}, u32[]{:S(2)}) async-start(bf16[4,4,120,768]{3,2,1,0:T(8,128)(2,1)} %bitcast.177), calls=%async_computation.2 | async-start | bytes 5898240 | tf_op jit(solution)/shard_map/all_to_all | solution.py:171
  173.6 281.9 %reduce-scatter.11.cloned.1.call-start = ((), (), s32[]{:S(2)}) async-start(), calls=%async_computation.12 | async-start | bytes 1327104 | tf_op jit(solution)/shard_map/reduce_scatter | solution.py:274
  266.5 37.1 %collective-permute-start.2 = (bf16[1,4,120,768]{3,2,1,0:T(8,128)(2,1)}, bf16[1,4,120,768]{3,2,1,0:T(8,128)(2,1)}, u32[]{:S(2)}, u32[]{:S(2)}) collective-permute-start(bf16[1,4,120,768]{3,2,1,0:T(8,128)(2,1)} %get-tuple-element.33), channel_id=1, source_target_pairs={{0,3},{1,2},{2,1},{3,0},{4,7},{5,6},{6,5},{7,4},{8,11},{9,10},{10,... | collective-permute-start | bytes 2211848 | tf_op jit(solution)/shard_map/ppermute | solution.py:24
  268.0 34.5 %collective-permute-start.1 = (bf16[1,4,120,768]{3,2,1,0:T(8,128)(2,1)}, bf16[1,4,120,768]{3,2,1,0:T(8,128)(2,1)}, u32[]{:S(2)}, u32[]{:S(2)}) collective-permute-start(bf16[1,4,120,768]{3,2,1,0:T(8,128)(2,1)} %get-tuple-element.34), channel_id=1, source_target_pairs={{0,2},{1,3},{2,0},{3,1},{4,6},{5,7},{6,4},{7,5},{8,10},{9,11},{10,... | collective-permute-start | bytes 2211848 | tf_op jit(solution)/shard_map/ppermute | solution.py:24
  269.5 31.8 %collective-permute-start = (bf16[1,4,120,768]{3,2,1,0:T(8,128)(2,1)}, bf16[1,4,120,768]{3,2,1,0:T(8,128)(2,1)}, u32[]{:S(2)}, u32[]{:S(2)}) collective-permute-start(bf16[1,4,120,768]{3,2,1,0:T(8,128)(2,1)} %get-tuple-element.35), channel_id=1, source_target_pairs={{0,1},{1,0},{2,3},{3,2},{4,5},{5,4},{6,7},{7,6},{8,9},{9,8},{10,11... | collective-permute-start | bytes 2211848 | tf_op jit(solution)/shard_map/ppermute | solution.py:24
  276.0 30.7 %copy-start.28 = (s32[2048]{0:T(1024)}, s32[2048]{0:T(1024)S(1)}, u32[]{:S(2)}) copy-start(s32[2048]{0:T(1024)S(1)} %pad_clamp_fusion.1) | copy-start | bytes 24580
  322.0 9.4 copy-start.31
  322.0 9.4 copy-start.36
  331.4 8.7 copy-start.2
  331.4 8.7 copy-start.6
  344.3 111.2 %reduce-scatter.13.cloned.1.call-start = ((), (), s32[]{:S(2)}) async-start(), calls=%async_computation.13 | async-start | bytes 3538944 | tf_op jit(solution)/shard_map/reduce_scatter | solution.py:280
  351.5 109.0 %reduce-scatter.15.cloned.1.call-start = ((), (), s32[]{:S(2)}) async-start(), calls=%async_computation.14 | async-start | bytes 3538944 | tf_op jit(solution)/shard_map/reduce_scatter | solution.py:283
  358.2 144.6 %reduce-scatter.17.cloned.1.call-start = ((), (), s32[]{:S(2)}) async-start(), calls=%async_computation.15 | async-start | bytes 3538944 | tf_op jit(solution)/shard_map/reduce_scatter | solution.py:286
  364.8 183.1 %reduce-scatter.9.cloned.1.call-start = ((), (), s32[]{:S(2)}) async-start(), calls=%async_computation.11 | async-start | bytes 3981312 | tf_op jit(solution)/shard_map/reduce_scatter | solution.py:271
  368.8 23.6 %copy-start.10 = (bf16[768,768]{0,1:T(8,128)(2,1)}, bf16[768,768]{0,1:T(8,128)(2,1)S(1)}, u32[]{:S(2)}) copy-start(bf16[768,768]{0,1:T(8,128)(2,1)S(1)} %convolution_convert_fusion.5) | copy-start | bytes 3538948
  416.5 9.9 copy-start.14
  455.5 238.1 %all-reduce.11.cloned.1.call-start = ((), (), s32[]{:S(2)}) async-start(), calls=%async_computation.19 | async-start | bytes 3538944 | tf_op jit(solution)/shard_map/psum | solution.py:292
  547.9 223.3 %reduce-scatter.23.cloned.1.call-start = ((), (), s32[]{:S(2)}) async-start(), calls=%async_computation.18 | async-start | bytes 14155776 | tf_op jit(solution)/shard_map/reduce_scatter | solution.py:202
  560.9 340.4 %reduce-scatter.19.cloned.1.call-start = ((), (), s32[]{:S(2)}) async-start(), calls=%async_computation.16 | async-start | bytes 14155776 | tf_op jit(solution)/shard_map/reduce_scatter | solution.py:196
  573.7 457.6 %reduce-scatter.21.cloned.1.call-start = ((), (), s32[]{:S(2)}) async-start(), calls=%async_computation.17 | async-start | bytes 14155776 | tf_op jit(solution)/shard_map/reduce_scatter | solution.py:199
  601.5 55.5 %all-to-all-start.1 = ((bf16[4,4,120,768]{3,2,1,0:T(8,128)(2,1)}), bf16[4,4,120,768]{3,2,1,0:T(8,128)(2,1)}, u32[]{:S(2)}, u32[]{:S(2)}) async-start(bf16[4,4,120,768]{3,2,1,0:T(8,128)(2,1)} %copy.52), calls=%async_computation.1 | async-start | bytes 5898240 | tf_op jit(solution)/shard_map/all_to_all | solution.py:160
  (28 other events, 102.2 us)
Sparse Core Ops, SparseCore 0:
  344.4 32.7 reduce-scatter.10
  379.6 38.5 reduce-scatter.12
  421.1 39.4 reduce-scatter.14
  463.3 39.4 reduce-scatter.16
  505.0 42.9 reduce-scatter.8
  551.9 87.5 all-reduce.10
  641.9 129.3 reduce-scatter.22
  773.6 127.5 reduce-scatter.18
  903.7 127.5 reduce-scatter.20
